TPU v7x, 32 devices: a whole 2x2x4 slice. The times are simulated.
32 devices in a mesh: seq: 8 (over z, y), tp: 4 (over x, core).
Axes of the slice: x: 2, y: 2, z: 4, core: 2. Of those that a mesh axis runs over, the one named last changes fastest.
Arguments:
- tokens: bfloat16 [6144, 4096], P('seq'), may hold values from -6 to 6
- query_weight: bfloat16 [4096, 2048], P('seq', 'tp'), may hold values from -0.09375 to 0.09375
- key_weight: bfloat16 [4096, 2048], P('seq', 'tp'), may hold values from -0.09375 to 0.09375
- value_weight: bfloat16 [4096, 2048], P('seq', 'tp'), may hold values from -0.09375 to 0.09375
- gate_weight: bfloat16 [4096, 16], P('seq', 'tp'), may hold values from -0.09375 to 0.09375
- decay_rate: float32 [16], P('tp'), may hold values from 3.2552085e-05 to 0.04
- norm_gain: float32 [2048], P('tp'), may hold values from 0.5 to 1.5
- out_weight: bfloat16 [2048, 4096], P(None, 'tp'), may hold values from -0.125 to 0.125
Outputs:
- mixed: bfloat16 [6144, 4096], P('seq', 'tp')
All inputs are finite; a program needn't handle non-finite values.
Results may differ from a plain program's by a relative error of at most 0.006.
The roundings to bfloat16 on the way count: a program that leaves them out, or rounds other values in their place, can miss the bound.
Values may be sent and summed in bfloat16 or wider, within the bound.
A program may use at most 128 MiB of HBM per device.

v0:
```python
import functools

import jax
import jax.numpy as jnp
from jax import lax
from jax.experimental import pallas as pl
from jax.experimental.pallas import tpu as pltpu
from jax.sharding import PartitionSpec as P

HALVES = 2
MESH = pl.DeviceIdType.MESH
CROSS = 2
PHASES = [[1, 0], [2], [4], [5], [3], [6], [7]]
EARLY = (2, 3, 5, 6, 7)
PARTS = 8


def layer_kernel(seq, tp, heads, wide, *refs):
    tok_in, rate_ref, gain_ref, gate_in, key_in, value_in, query_in, out_in = refs[:8]
    mixed_ref = refs[8]
    gate_buf, kvq_buf, gate_acc, acc, out_buf, out_acc, wcol, wrow = refs[9:17]
    state_mine, state_wire, state_peer, total_mine, total_peer = refs[17:22]
    state_in, state_next, state_pre, normed_buf, tok_ref = refs[22:27]
    gate_raw = refs[41]
    own_sem, send_own, send_line, send_peer, recv_sem = refs[27:32]
    tok_send, tok_recv, local_send, local_recv, state_send, state_recv = refs[32:38]
    normed_send, normed_recv, guest_send = refs[38:41]
    rows = key_in.shape[0]
    half = key_in.shape[1] // HALVES
    quarter = half // 2
    line = seq // CROSS
    me = lax.axis_index("seq")
    a, b = me // CROSS, me % CROSS
    peer = a * CROSS + (1 - b)
    count = acc.shape[1] // 2
    head_size = 2 * half // heads
    per_half = heads // HALVES
    block = 256 if count % 256 == 0 else count
    blocks = count // block
    col = lax.axis_index("tp")
    pair_col = col + 1 - 2 * (col % 2)
    groups = tp // 2
    last = line - 1
    is_end = (a == 0) | (a == last)
    is_worker = (a > 0) & (a < last)
    all_hosts = line == 4
    is_host = (a == 1) | (a == last - 1)
    is_low = a == 1
    up_works, down_works = a + 1 < last, a - 1 > 0
    partner = jnp.where((a == 0) | ((a == last - 1) & (a != 1)), me + CROSS, me - CROSS)
    units = [
        (0, 0, half, range(per_half)),
        (1, 0, quarter, range(per_half // 2)),
        (1, quarter, quarter, range(per_half // 2, per_half)),
    ]

    def hosts(run):
        if all_hosts:
            run()
        else:
            pl.when(is_host)(run)

    def buffer(piece, source):
        if piece == 0:
            return gate_buf.at[source]
        if piece >= 3 * HALVES:
            at = pl.ds((piece - 3 * HALVES) * quarter, quarter)
            return kvq_buf.at[3 * HALVES - 1, source, :, at]
        return kvq_buf.at[piece - 1, source]

    def copy(piece, source, sem, target):
        return pltpu.make_async_remote_copy(
            src_ref=buffer(piece, source),
            dst_ref=buffer(piece, source),
            send_sem=sem,
            recv_sem=recv_sem.at[piece, source],
            device_id={"seq": target},
            device_id_type=MESH,
        )

    def arrive(piece, source):
        copy(piece, source, send_own.at[piece, 0], peer).wait_recv()

    loads = [pltpu.make_async_copy(gate_in, gate_raw, own_sem.at[0])]
    for index in range(3 * HALVES):
        source_ref = (key_in, value_in, query_in)[index % 3]
        at = (index // 3) * half
        loads.append(
            pltpu.make_async_copy(
                source_ref.at[:, pl.ds(at, half)], kvq_buf.at[index, me], own_sem.at[index + 1]
            )
        )
    for load in loads:
        load.start()
    if wide:
        own_tok = tok_ref.at[pl.ds(0, count), :]
    else:
        own_tok = tok_ref.at[:, pl.ds(0, count), :]
    tok_load = pltpu.make_async_copy(tok_in, own_tok, own_sem.at[3 * HALVES + 2])
    pl.when(is_worker)(tok_load.start)
    out_load = pltpu.make_async_copy(out_in, out_buf, own_sem.at[3 * HALVES + 1])
    out_load.start()

    barrier = pltpu.get_barrier_semaphore()
    has_up, has_down = a < last, a > 0
    pl.semaphore_signal(barrier, inc=1, device_id={"seq": peer}, device_id_type=MESH)

    @pl.when(has_up)
    def _():
        pl.semaphore_signal(barrier, inc=1, device_id={"seq": me + CROSS}, device_id_type=MESH)

    @pl.when(has_down)
    def _():
        pl.semaphore_signal(barrier, inc=1, device_id={"seq": me - CROSS}, device_id_type=MESH)

    pl.semaphore_signal(barrier, inc=1, device_id={"tp": pair_col}, device_id_type=MESH)
    for g in range(1, groups):
        pl.semaphore_signal(
            barrier, inc=1, device_id={"tp": lax.rem(col + 2 * g, tp)}, device_id_type=MESH
        )
    pl.semaphore_wait(barrier, 1 + groups + has_up.astype(jnp.int32) + has_down.astype(jnp.int32))

    def load_wait(piece):
        if piece <= 3 * HALVES:
            loads[piece].wait()
        if piece == 0:
            raw = gate_raw[...].astype(jnp.float32)
            raw = jnp.concatenate([raw, jnp.zeros((rows, 128 - heads), jnp.float32)], axis=1)
            gate_buf[me] = raw.T[:16].astype(jnp.bfloat16)

    def ready(number):
        for piece in PHASES[number]:
            load_wait(piece)

    def far(g):
        return lax.rem(col + 2 * g, tp)

    def far_pair(g):
        return lax.rem(pair_col + 2 * g, tp)

    def own_line(number):
        for piece in PHASES[number]:

            @pl.when(up_works)
            def _():
                copy(piece, me, send_own.at[piece, 1], me + CROSS).start()

            @pl.when(down_works)
            def _():
                copy(piece, me, send_own.at[piece, 2], me - CROSS).start()

    def own_cross(number):
        for piece in PHASES[number]:
            copy(piece, me, send_own.at[piece, 0], peer).start()

    def each_middle(run):
        @pl.loop(0, 2 * (line - 3))
        def _(n):
            sign = 1 - 2 * (n % 2)
            origin = a - sign * (1 + n // 2)
            onward = (a + sign > 0) & (a + sign < last)

            @pl.when((origin > 0) & (origin < last))
            def _():
                run(origin, onward, me + sign * CROSS)

    near_low = 2 * a < line
    near_origin = jnp.where(near_low, 0, last)
    far_origin = last - near_origin
    near_onward = jnp.where(near_low, up_works, down_works)
    far_onward = jnp.where(near_low, down_works, up_works)
    away = jnp.where(near_low, CROSS, -CROSS)

    def ends():
        return (near_origin, near_onward, me + away), (far_origin, far_onward, me - away)

    def middle(number):
        def run(origin, onward, target):
            source = origin * CROSS + b
            for piece in PHASES[number]:
                arrive(piece, source)
                copy(piece, source, send_peer.at[piece, source], peer).start()

                @pl.when(onward)
                def _():
                    copy(piece, source, send_line.at[piece, source], target).start()

        each_middle(run)

    def outer(number, which, side):
        origin, onward, target = ends()[which]
        source = origin * CROSS + (b if side == 0 else 1 - b)
        for piece in PHASES[number]:
            arrive(piece, source)

            @pl.when(onward)
            def _():
                copy(piece, source, send_line.at[piece, source], target).start()

            if piece not in EARLY:
                copy(piece, source, send_peer.at[piece, source], peer).start()

    def tok_part(ref, index, base):
        if wide:
            size = ref.shape[1] // (tp * PARTS)
            at = pl.ds(pl.multiple_of(index * size, size), size)
            return ref.at[pl.ds(base, count), at]
        size = seq // (tp * PARTS)
        return ref.at[pl.ds(index * size, size), pl.ds(base, count), :]

    def tok_copy(index, j, send, target, first=False):
        return pltpu.make_async_remote_copy(
            src_ref=tok_part(tok_in, index, 0) if first else tok_part(tok_ref, index, count),
            dst_ref=tok_part(tok_ref, index, count),
            send_sem=tok_send.at[j, send],
            recv_sem=tok_recv.at[index],
            device_id=target,
            device_id_type=MESH,
        )

    def tok_arrive(index):
        tok_copy(index, 0, 0, {"tp": pair_col}).wait_recv()

    def tok_spread(j):
        def run():
            index = col * PARTS + j
            tok_arrive(index)
            for g in range(1, groups):
                tok_copy(index, j, g, {"tp": far(g)}).start()
            tok_copy(index, j, 0, {"tp": pair_col}).start()

        hosts(run)

    def tok_relay(j):
        def run():
            for g in range(1, groups):
                index = far(g) * PARTS + j
                tok_arrive(index)
                tok_copy(index, j, groups - 1 + g, {"tp": pair_col}).start()

        hosts(run)

    def tok_rest():
        def run():
            for j in range(PARTS):
                tok_arrive(pair_col * PARTS + j)
                for g in range(1, groups):
                    tok_arrive(far_pair(g) * PARTS + j)

        hosts(run)

    def multiply(piece, source, base, size):
        at = slice(base, base + size)
        if wide:
            x = tok_ref[at, pl.ds(pl.multiple_of(source * rows, rows), rows)]
        else:
            x = tok_ref[source, at]
        if piece == 0:
            gate_acc[at] += lax.dot_general(
                x, gate_buf[source], (((1,), (1,)), ((), ())), preferred_element_type=jnp.float32
            )
        elif piece >= 3 * HALVES:
            cols = slice((piece - 3 * HALVES) * quarter, (piece - 3 * HALVES + 1) * quarter)
            acc[3 * HALVES - 1, at, cols] += jnp.dot(
                x, kvq_buf[3 * HALVES - 1, source, :, cols], preferred_element_type=jnp.float32
            )
        else:
            acc[piece - 1, at] += jnp.dot(
                x, kvq_buf[piece - 1, source], preferred_element_type=jnp.float32
            )

    def product(piece, source, part):
        if part == "own":
            multiply(piece, source, 0, count)
        elif part == "guest":
            hosts(lambda: multiply(piece, source, count, count))
        elif all_hosts:
            multiply(piece, source, 0, 2 * count)
        else:

            @pl.when(is_host)
            def _():
                multiply(piece, source, 0, 2 * count)

            @pl.when(jnp.logical_not(is_host))
            def _():
                multiply(piece, source, 0, count)

    def mine(number, part):
        for piece in PHASES[number]:
            product(piece, me, part)

    def middles(number, part):
        def run(origin, onward, target):
            for piece in PHASES[number]:
                product(piece, origin * CROSS + b, part)

        each_middle(run)

    def outside(number, which, part):
        origin = ends()[which][0]
        for piece in PHASES[number]:
            if piece in EARLY:

                @pl.loop(0, CROSS)
                def _(side):
                    product(piece, origin * CROSS + side, part)

            else:
                product(piece, origin * CROSS + b, part)

    def crossed_mine(number, part):
        for piece in PHASES[number]:
            arrive(piece, peer)
            product(piece, peer, part)

    def crossed(number, part):
        pieces = PHASES[number]

        def run(origin, onward, target):
            for piece in pieces:
                source = origin * CROSS + (1 - b)
                arrive(piece, source)
                product(piece, source, part)

        each_middle(run)

    def crossed_outside(number, which, part):
        for piece in PHASES[number]:
            if piece not in EARLY:
                source = ends()[which][0] * CROSS + (1 - b)
                arrive(piece, source)
                product(piece, source, part)

    def guests(number, rest=True):
        pieces = PHASES[number]

        def run():
            if rest:

                @pl.loop(0, seq)
                def _(source):
                    for piece in pieces:
                        multiply(piece, source, count, count)

            else:

                @pl.loop(CROSS, seq - CROSS)
                def _(source):
                    for piece in pieces:
                        multiply(piece, source, count, count)

        hosts(run)

    trips = 2 if all_hosts else 1 + is_host.astype(jnp.int32)
    first_group = jnp.where(is_low, 1, 0)
    second_group = 1 - first_group

    def token_rows(w, start, size):
        return pl.ds(pl.multiple_of(w * count + start, block), size)

    def decays():
        @pl.loop(0, trips)
        def _(w):
            logits = jnp.concatenate(
                [
                    gate_acc[token_rows(w, 0, count)],
                    jnp.zeros((count, 128 - gate_acc.shape[1]), jnp.float32),
                ],
                axis=1,
            ).T[:8]
            soft = jnp.maximum(logits, 0.0) + jnp.log1p(jnp.exp(-jnp.abs(logits)))
            head_row = lax.broadcasted_iota(jnp.int32, soft.shape, 0)
            rate = jnp.zeros(soft.shape, jnp.float32)
            for head in range(heads):
                rate = jnp.where(head_row == head, rate_ref[head], rate)
            total = -rate * soft
            lane = lax.broadcasted_iota(jnp.int32, total.shape, 1)
            reach = 1
            while reach < count:
                total = total + jnp.where(lane >= reach, pltpu.roll(total, reach, 1), 0.0)
                reach *= 2
            wrow[w] = total
            wcol[w] = jnp.concatenate([total, jnp.zeros((120, count), jnp.float32)], axis=0).T

    class local_copy:
        def __init__(self, h, slot, group):
            pairs = ((state_wire, state_peer), (total_mine, total_peer))
            self.copies = [
                pltpu.make_async_remote_copy(
                    src_ref=source.at[group, h],
                    dst_ref=target.at[slot, h],
                    send_sem=local_send.at[n, slot, h],
                    recv_sem=local_recv.at[n, slot, h],
                    device_id={"seq": peer},
                    device_id_type=MESH,
                )
                for n, (source, target) in enumerate(pairs)
            ]

        def start(self):
            for one in self.copies:
                one.start()

        def wait_recv(self):
            for one in self.copies:
                one.wait_recv()

        def wait_send(self):
            for one in self.copies:
                one.wait_send()

    def local_state(h):
        @pl.loop(0, trips)
        def _(w):
            for j in range(per_half):
                head = h * per_half + j
                cols = slice(j * head_size, (j + 1) * head_size)
                within = wcol[w, :, head : head + 1]
                final = wcol[w, count - 1 : count, head : head + 1]
                at = token_rows(w, 0, count)
                key = acc[3 * h, at, cols].astype(jnp.bfloat16).astype(jnp.float32)
                scaled = (jnp.exp(final - within) * key).astype(jnp.bfloat16)
                value = acc[3 * h + 1, at, cols].astype(jnp.bfloat16)
                local = lax.dot_general(
                    scaled, value, (((0,), (0,)), ((), ())), preferred_element_type=jnp.float32
                )
                state_mine[w, h, j * head_size : (j + 1) * head_size] = local
                state_wire[w, h, j * head_size : (j + 1) * head_size] = local.astype(jnp.bfloat16)
                total_mine[w, h, j : j + 1] = jnp.broadcast_to(final, (1, head_size))

        local_copy(h, 0, first_group).start()
        hosts(lambda: local_copy(h, 1, second_group).start())

    def line_state(h):
        return pltpu.make_async_remote_copy(
            src_ref=state_next.at[h],
            dst_ref=state_in.at[h],
            send_sem=state_send.at[h],
            recv_sem=state_recv.at[h],
            device_id={"seq": me + CROSS},
            device_id_type=MESH,
        )

    def chain(h):
        @pl.when(is_low)
        def _():
            state_in[h] = jnp.zeros(state_in.shape[1:], jnp.float32)

        @pl.when(jnp.logical_not(is_low))
        def _():
            line_state(h).wait_recv()

        spans = [slice(j * head_size, (j + 1) * head_size) for j in range(per_half)]

        def step(state, j, slot, group, peers):
            own = (total_mine[group, h, j : j + 1], state_mine[group, h, spans[j]])
            other = (
                total_peer[slot, h, j : j + 1],
                state_peer[slot, h, spans[j]].astype(jnp.float32),
            )
            total = jnp.where(peers, other[0], own[0])
            return jnp.exp(total) * state + jnp.where(peers, other[1], own[1])

        def pass_group(slot, group):
            local_copy(h, slot, group).wait_recv()
            for j, at in enumerate(spans):
                state = state_in[h, at] if slot == 0 else state_next[h, at]
                middle_state = step(state, j, slot, group, b == 1)
                state_pre[group, h, at] = jnp.where(b == 1, middle_state, state).astype(
                    jnp.bfloat16
                )
                state_next[h, at] = step(middle_state, j, slot, group, b == 0)

        pass_group(0, first_group)
        hosts(lambda: pass_group(1, second_group))

        @pl.when(up_works)
        def _():
            line_state(h).start()

    def block_rows(i):
        return pl.ds(i * block if isinstance(i, int) else pl.multiple_of(i * block, block), block)

    def normed_copy(u, i, source, send, target):
        h, start, size, _ = units[u]
        ref = normed_buf.at[h, source, block_rows(i), pl.ds(start, size)]
        return pltpu.make_async_remote_copy(
            src_ref=ref,
            dst_ref=ref,
            send_sem=normed_send.at[u, i, send],
            recv_sem=normed_recv.at[u, i, source],
            device_id={"tp": target},
            device_id_type=MESH,
        )

    def guest_copy(u, i):
        h, start, size, _ = units[u]
        return pltpu.make_async_remote_copy(
            src_ref=normed_buf.at[h, tp, block_rows(i), pl.ds(start, size)],
            dst_ref=normed_buf.at[h, col, block_rows(i), pl.ds(start, size)],
            send_sem=guest_send.at[u, i],
            recv_sem=normed_recv.at[u, i, col],
            device_id={"seq": partner},
            device_id_type=MESH,
        )

    def share(u, i):
        for g in range(1, groups):
            normed_copy(u, i, col, g, far(g)).start()
        normed_copy(u, i, col, 0, pair_col).start()

    def relay(u, i):
        for g in range(1, groups):
            normed_copy(u, i, far(g), 0, pair_col).wait_recv()
            normed_copy(u, i, far(g), groups - 1 + g, pair_col).start()

    def attention(u):
        h, _, _, members = units[u]

        @pl.loop(0, trips)
        def _(n):
            w = trips - 1 - n
            slot = jnp.where(w == 0, col, tp)
            for i in range(blocks):
                upto = (i + 1) * block
                row = i * block + lax.broadcasted_iota(jnp.int32, (block, upto), 0)
                causal = lax.broadcasted_iota(jnp.int32, (block, upto), 1) <= row
                t_at = token_rows(w, i * block, block)
                s_at = token_rows(w, 0, upto)
                for j in members:
                    head = h * per_half + j
                    cols = slice(j * head_size, (j + 1) * head_size)
                    query = acc[3 * h + 2, t_at, cols].astype(jnp.bfloat16)
                    key = acc[3 * h, s_at, cols].astype(jnp.bfloat16)
                    value = acc[3 * h + 1, s_at, cols].astype(jnp.bfloat16)
                    within = wcol[w, i * block : (i + 1) * block, head : head + 1]
                    scores = lax.dot_general(
                        query, key, (((1,), (1,)), ((), ())), preferred_element_type=jnp.float32
                    )
                    gap = within - wrow[w, head : head + 1, :upto]
                    attn = jnp.where(causal, scores * jnp.exp(jnp.where(causal, gap, 0.0)), 0.0)
                    local = jnp.dot(
                        attn.astype(jnp.bfloat16), value, preferred_element_type=jnp.float32
                    )
                    scaled = (jnp.exp(within) * query.astype(jnp.float32)).astype(jnp.bfloat16)
                    state = state_pre[w, h, j * head_size : (j + 1) * head_size]
                    head_out = local + jnp.dot(scaled, state, preferred_element_type=jnp.float32)
                    square = jnp.mean(head_out * head_out, axis=-1, keepdims=True)
                    gain = gain_ref[:, head * head_size : (head + 1) * head_size]
                    normed_buf[h, slot, i * block : (i + 1) * block, cols] = (
                        head_out * lax.rsqrt(square + 1e-05) * gain
                    ).astype(jnp.bfloat16)

                @pl.when(w == 0)
                def _():
                    share(u, i)

                @pl.when(w == 1)
                def _():
                    guest_copy(u, i).start()

    def settle(h):
        mine = [u for u in range(len(units)) if units[u][0] == h]

        def mix(i, source):
            depth = pl.ds(pl.multiple_of((source * HALVES + h) * half, half), half)
            return jnp.dot(
                normed_buf[h, source, block_rows(i)],
                out_buf[depth, :],
                preferred_element_type=jnp.float32,
            )

        @pl.loop(0, blocks)
        def _(i):
            at = block_rows(i)
            total = mix(i, col)
            for u in mine:
                normed_copy(u, i, pair_col, 0, pair_col).wait_recv()
            total = total + mix(i, pair_col)
            for g in range(1, groups):
                total = total + mix(i, far(g))
                for u in mine:
                    normed_copy(u, i, far_pair(g), 0, pair_col).wait_recv()
                total = total + mix(i, far_pair(g))
            if h == 0:
                out_acc[at, :] = total
            else:
                mixed_ref[at, :] = (out_acc[at, :] + total).astype(jnp.bfloat16)

    def relays(u):
        @pl.loop(0, blocks)
        def _(i):
            relay(u, i)

    @pl.when(is_end)
    def _():
        for j in range(PARTS):
            tok_copy(col * PARTS + j, j, 0, {"seq": partner}, True).start()
        for pieces in PHASES:
            for piece in pieces:
                load_wait(piece)
                if piece in EARLY:
                    copy(piece, me, send_own.at[piece, 0], peer).start()
        for pieces in PHASES:
            for piece in pieces:
                copy(piece, me, send_own.at[piece, 1], partner).start()
                if piece in EARLY:
                    arrive(piece, peer)
                    copy(piece, peer, send_line.at[piece, peer], partner).start()
        out_load.wait()

        def hand_out(u):
            @pl.loop(0, blocks)
            def _(i):
                guest_copy(u, i).wait_recv()
                share(u, i)

        hand_out(0)
        hand_out(1)
        relays(0)
        hand_out(2)
        relays(1)
        settle(0)
        relays(2)

    @pl.when(is_worker)
    def _():
        gate_acc[...] = jnp.zeros_like(gate_acc)
        acc[...] = jnp.zeros_like(acc)
        ready(0)
        own_cross(0)
        own_line(0)
        tok_spread(0)
        ready(1)
        own_cross(1)
        own_line(1)
        tok_spread(1)
        middle(0)
        tok_relay(0)
        middle(1)
        tok_spread(2)
        ready(2)
        own_line(2)
        tok_spread(3)
        own_cross(2)
        tok_spread(4)
        ready(4)
        tok_load.wait()
        mine(4, "own")
        ready(3)
        own_cross(3)
        own_line(3)
        crossed_mine(1, "own")
        tok_relay(1)
        own_line(4)
        middle(2)
        tok_relay(2)
        ready(5)
        own_line(5)
        tok_spread(5)
        crossed(0, "own")
        middles(0, "own")
        ready(6)
        own_line(6)
        tok_relay(3)
        middle(3)
        tok_spread(6)
        outer(0, 0, 0)
        mine(5, "own")
        tok_spread(7)
        crossed_mine(2, "own")
        tok_relay(4)
        tok_relay(5)
        mine(1, "own")
        outer(1, 0, 0)
        crossed(1, "own")
        tok_relay(6)
        mine(6, "own")
        tok_relay(7)
        outer(0, 1, 0)
        own_cross(4)
        middles(3, "own")
        middles(2, "own")
        mine(3, "own")
        crossed(3, "own")
        crossed_mine(0, "own")
        tok_rest()
        outer(1, 0, 1)
        outside(1, 0, "both")
        guests(1, False)
        crossed_mine(3, "own")
        outside(0, 1, "own")
        crossed_outside(0, 0, "own")
        outer(2, 0, 0)
        guests(3, False)
        outside(0, 0, "own")
        mine(2, "own")
        outer(1, 1, 1)
        crossed_outside(0, 1, "own")
        outer(1, 1, 0)
        outside(1, 1, "both")
        outer(3, 0, 0)
        guests(0)
        outside(2, 0, "own")
        middles(1, "own")
        mine(0, "own")
        crossed(2, "own")
        outer(2, 1, 0)
        outside(2, 1, "own")
        outer(3, 0, 1)
        decays()
        middle(4)
        crossed_mine(4, "own")
        middles(4, "own")
        local_state(0)
        middle(5)
        crossed_outside(2, 0, "own")
        outer(3, 1, 0)
        middles(5, "own")
        outer(4, 0, 0)
        middle(6)
        outside(3, 0, "both")
        crossed_outside(2, 1, "own")
        guests(2)
        outer(4, 0, 1)
        outside(4, 0, "both")
        outer(3, 1, 1)
        crossed(4, "own")
        outside(3, 1, "both")
        local_state(1)
        outer(4, 1, 0)
        middles(6, "own")
        own_cross(5)
        chain(0)
        guests(4, False)
        own_cross(6)
        outer(5, 0, 0)
        outer(5, 0, 1)
        outer(4, 1, 1)
        outside(4, 1, "both")
        attention(0)
        outside(5, 0, "both")
        chain(1)
        outer(6, 0, 0)
        crossed_mine(5, "own")
        outer(6, 0, 1)
        outside(6, 0, "both")
        crossed_mine(6, "own")
        outer(5, 1, 1)
        outer(5, 1, 0)
        outside(5, 1, "both")
        crossed(5, "own")
        guests(5, False)
        attention(1)
        crossed(6, "own")
        guests(6, False)
        outer(6, 1, 1)
        outer(6, 1, 0)
        outside(6, 1, "both")
        attention(2)
        relays(0)
        relays(1)
        out_load.wait()
        settle(0)
        relays(2)

    settle(1)

    @pl.loop(0, blocks)
    def _(i):
        for u in range(len(units)):
            for k in range(tp - 1):
                normed_copy(u, i, col, k, pair_col).wait_send()

    @pl.when(is_end)
    def _():
        for pieces in PHASES:
            for piece in pieces:
                copy(piece, me, send_own.at[piece, 1], peer).wait_send()
                if piece in EARLY:
                    copy(piece, me, send_own.at[piece, 0], peer).wait_send()
                    copy(piece, peer, send_line.at[piece, peer], peer).wait_send()
        for j in range(PARTS):
            tok_copy(col * PARTS + j, j, 0, {"seq": partner}, True).wait_send()

    @pl.when(is_worker)
    def _():
        def host_drain():
            for j in range(PARTS):
                for k in range(tp - 1):
                    tok_copy(col * PARTS + j, j, k, {"tp": pair_col}).wait_send()

            @pl.loop(0, blocks)
            def _(i):
                for u in range(len(units)):
                    guest_copy(u, i).wait_send()

        hosts(host_drain)
        for h in range(HALVES):

            local_copy(h, 0, first_group).wait_send()
            hosts(lambda: local_copy(h, 1, second_group).wait_send())

            @pl.when(up_works)
            def _():
                line_state(h).wait_send()

        for pieces in PHASES:
            for piece in pieces:
                copy(piece, me, send_own.at[piece, 0], peer).wait_send()

                @pl.when(up_works)
                def _():
                    copy(piece, me, send_own.at[piece, 1], peer).wait_send()

                @pl.when(down_works)
                def _():
                    copy(piece, me, send_own.at[piece, 2], peer).wait_send()

                for origin, onward, _ in ends():
                    source, other = origin * CROSS + b, origin * CROSS + (1 - b)

                    @pl.when(onward)
                    def _():
                        copy(piece, source, send_line.at[piece, source], peer).wait_send()
                        if piece in EARLY:
                            copy(piece, other, send_line.at[piece, other], peer).wait_send()

                    if piece not in EARLY:
                        copy(piece, source, send_peer.at[piece, source], peer).wait_send()

        def run(origin, onward, target):
            source = origin * CROSS + b
            for pieces in PHASES:
                for piece in pieces:
                    copy(piece, source, send_peer.at[piece, source], peer).wait_send()

                    @pl.when(onward)
                    def _():
                        copy(piece, source, send_line.at[piece, source], peer).wait_send()

        each_middle(run)


def on_device(
    seq,
    tp,
    tokens,
    query_weight,
    key_weight,
    value_weight,
    gate_weight,
    decay_rate,
    norm_gain,
    out_weight,
):
    count = tokens.shape[0]
    rows, width = query_weight.shape
    heads = gate_weight.shape[1]
    half = width // HALVES
    head_size = width // heads
    wide = rows % 128 == 0
    tok = tokens if wide else tokens.reshape(count, seq, rows).transpose(1, 0, 2)
    vmem = pl.BlockSpec(memory_space=pltpu.VMEM)
    smem = pl.BlockSpec(memory_space=pltpu.SMEM)
    hbm = pl.BlockSpec(memory_space=pl.ANY)
    pieces = 3 * HALVES + 2
    blocks = count // 256 if count % 256 == 0 else 1
    dma = pltpu.SemaphoreType.DMA
    deep = head_size * heads // HALVES
    out_width = out_weight.shape[1]
    both = (2 * count, tok.shape[1]) if wide else (seq, 2 * count, rows)
    return pl.pallas_call(
        functools.partial(layer_kernel, seq, tp, heads, wide),
        out_shape=jax.ShapeDtypeStruct((count, out_width), jnp.bfloat16),
        in_specs=[hbm, smem, vmem, hbm, hbm, hbm, hbm, hbm],
        out_specs=vmem,
        scratch_shapes=[
            pltpu.VMEM((seq, 16, rows), jnp.bfloat16),
            pltpu.VMEM((3 * HALVES, seq, rows, half), jnp.bfloat16),
            pltpu.VMEM((2 * count, 16), jnp.float32),
            pltpu.VMEM((3 * HALVES, 2 * count, half), jnp.float32),
            pltpu.VMEM(out_weight.shape, jnp.bfloat16),
            pltpu.VMEM((count, out_width), jnp.float32),
            pltpu.VMEM((2, count, 128), jnp.float32),
            pltpu.VMEM((2, 8, count), jnp.float32),
            pltpu.VMEM((2, HALVES, deep, head_size), jnp.float32),
            pltpu.VMEM((2, HALVES, deep, head_size), jnp.bfloat16),
            pltpu.VMEM((2, HALVES, deep, head_size), jnp.bfloat16),
            pltpu.VMEM((2, HALVES, 8, head_size), jnp.float32),
            pltpu.VMEM((2, HALVES, 8, head_size), jnp.float32),
            pltpu.VMEM((HALVES, deep, head_size), jnp.float32),
            pltpu.VMEM((HALVES, deep, head_size), jnp.float32),
            pltpu.VMEM((2, HALVES, deep, head_size), jnp.bfloat16),
            pltpu.VMEM((HALVES, tp + 1, count, half), jnp.bfloat16),
            pltpu.VMEM(both, jnp.bfloat16),
            dma((pieces + 2,)),
            dma((pieces, 3)),
            dma((pieces, seq)),
            dma((pieces, seq)),
            dma((pieces, seq)),
            dma((PARTS, tp - 1)),
            dma((tp * PARTS,)),
            dma((2, 2, HALVES)),
            dma((2, 2, HALVES)),
            dma((HALVES,)),
            dma((HALVES,)),
            dma((3, blocks, tp - 1)),
            dma((3, blocks, tp)),
            dma((3, blocks)),
            pltpu.VMEM((rows, heads), jnp.bfloat16),
        ],
        compiler_params=pltpu.CompilerParams(
            collective_id=0, has_side_effects=True, vmem_limit_bytes=62 * 1024 * 1024
        ),
    )(tok, decay_rate, norm_gain[None, :], gate_weight, key_weight, value_weight, query_weight, out_weight)


def solution(mesh):
    return jax.shard_map(
        functools.partial(on_device, mesh.shape["seq"], mesh.shape["tp"]),
        mesh=mesh,
        in_specs=(
            P("seq", None),
            P("seq", "tp"),
            P("seq", "tp"),
            P("seq", "tp"),
            P("seq", "tp"),
            P("tp"),
            P("tp"),
            P(None, "tp"),
        ),
        out_specs=P("seq", "tp"),
        check_vma=False,
    )
```

profile of v0, /device:TPU:0, one launch (start us, length us, event | category | flops | bytes accessed | tf_op | source)
XLA Modules:
  0.0 134.5 jit_solution(2608890836500177110)
XLA Ops:
  0.0 1.5 %copy.9.refs_3_ = bf16[512,4]{1,0:T(8,128)(2,1)} copy(bf16[512,4]{0,1:T(4,128)(2,1)} %param.12) | data formatting | bytes 8192 | tf_op args[4]
  1.5 130.3 %shard_map.82 = bf16[768,1024]{1,0:T(8,128)(2,1)} custom-call(bf16[768,4096]{1,0:T(8,128)(2,1)} %refs_0_.1, f32[4]{0:T(128)} %refs_1_.1, f32[1,512]{1,0:T(1,128)} %bitcast.1, bf16[512,4]{1,0:T(8,128)(2,1)} %copy.9.refs_3_, bf16[512,512]{1,0:T(8,128)(2,1)} %refs_4_.1, bf16[512,512]{1,0:T(8,128)(2,1)} %refs_5_.1, bf16[512,512]{1,0:T(8,128)(2,1)} %refs_6_.1, ...), custom_call_target="tpu_custom_call" | custom-call | tf_op jit(solution)/shard_map/pallas_call | solution.py:874
  131.8 2.7 %copy.11 = bf16[768,1024]{1,0:T(8,128)(2,1)} copy(bf16[768,1024]{1,0:T(8,128)(2,1)} %shard_map.82) | data formatting | bytes 3145728
where the time goes:
time: 135 us; the launch traced here: 134 us
  Pallas kernels  130 us (96%)
  local copies, waits for them, and re-layouts  4.17 us (3%)
    pallas_call x1, Pallas kernels, on_device(): pl.pallas_call(functools.partial(layer_kernel, seq, tp, heads, wide), out...  130 us
    unnamed x2, local copies, waits for them, and re-layouts  4.17 us

commit v1 on v0

--- a/solution.py
+++ b/solution.py
@@ -442,13 +442,13 @@
             device_id_type=MESH,
         )
 
-    def chain(h):
-        @pl.when(is_low)
-        def _():
+    def chain(h, low):
+        pl.when(is_low if low else jnp.logical_not(is_low))(lambda: chain_step(h, low))
+
+    def chain_step(h, low):
+        if low:
             state_in[h] = jnp.zeros(state_in.shape[1:], jnp.float32)
-
-        @pl.when(jnp.logical_not(is_low))
-        def _():
+        else:
             line_state(h).wait_recv()
 
         spans = [slice(j * head_size, (j + 1) * head_size) for j in range(per_half)]
@@ -593,6 +593,68 @@
         def _(i):
             relay(u, i)
 
+    def end_drain():
+        for pieces in PHASES:
+            for piece in pieces:
+                copy(piece, me, send_own.at[piece, 1], peer).wait_send()
+                if piece in EARLY:
+                    copy(piece, me, send_own.at[piece, 0], peer).wait_send()
+                    copy(piece, peer, send_line.at[piece, peer], peer).wait_send()
+        for j in range(PARTS):
+            tok_copy(col * PARTS + j, j, 0, {"seq": partner}, True).wait_send()
+
+    def worker_drain():
+        def host_drain():
+            for j in range(PARTS):
+                for k in range(tp - 1):
+                    tok_copy(col * PARTS + j, j, k, {"tp": pair_col}).wait_send()
+
+        hosts(host_drain)
+        for h in range(HALVES):
+
+            local_copy(h, 0, first_group).wait_send()
+            hosts(lambda: local_copy(h, 1, second_group).wait_send())
+
+            @pl.when(up_works)
+            def _():
+                line_state(h).wait_send()
+
+        for pieces in PHASES:
+            for piece in pieces:
+                copy(piece, me, send_own.at[piece, 0], peer).wait_send()
+
+                @pl.when(up_works)
+                def _():
+                    copy(piece, me, send_own.at[piece, 1], peer).wait_send()
+
+                @pl.when(down_works)
+                def _():
+                    copy(piece, me, send_own.at[piece, 2], peer).wait_send()
+
+                for origin, onward, _ in ends():
+                    source, other = origin * CROSS + b, origin * CROSS + (1 - b)
+
+                    @pl.when(onward)
+                    def _():
+                        copy(piece, source, send_line.at[piece, source], peer).wait_send()
+                        if piece in EARLY:
+                            copy(piece, other, send_line.at[piece, other], peer).wait_send()
+
+                    if piece not in EARLY:
+                        copy(piece, source, send_peer.at[piece, source], peer).wait_send()
+
+        def run(origin, onward, target):
+            source = origin * CROSS + b
+            for pieces in PHASES:
+                for piece in pieces:
+                    copy(piece, source, send_peer.at[piece, source], peer).wait_send()
+
+                    @pl.when(onward)
+                    def _():
+                        copy(piece, source, send_line.at[piece, source], peer).wait_send()
+
+        each_middle(run)
+
     @pl.when(is_end)
     def _():
         for j in range(PARTS):
@@ -619,6 +681,7 @@
         hand_out(0)
         hand_out(1)
         relays(0)
+        end_drain()
         hand_out(2)
         relays(1)
         settle(0)
@@ -626,8 +689,6 @@
 
     @pl.when(is_worker)
     def _():
-        gate_acc[...] = jnp.zeros_like(gate_acc)
-        acc[...] = jnp.zeros_like(acc)
         ready(0)
         own_cross(0)
         own_line(0)
@@ -646,6 +707,8 @@
         own_cross(2)
         tok_spread(4)
         ready(4)
+        gate_acc[...] = jnp.zeros_like(gate_acc)
+        acc[...] = jnp.zeros_like(acc)
         tok_load.wait()
         mine(4, "own")
         ready(3)
@@ -732,16 +795,17 @@
         outer(4, 1, 0)
         middles(6, "own")
         own_cross(5)
-        chain(0)
         guests(4, False)
         own_cross(6)
+        chain(0, True)
         outer(5, 0, 0)
         outer(5, 0, 1)
         outer(4, 1, 1)
         outside(4, 1, "both")
+        chain(0, False)
         attention(0)
+        chain(1, True)
         outside(5, 0, "both")
-        chain(1)
         outer(6, 0, 0)
         crossed_mine(5, "own")
         outer(6, 0, 1)
@@ -752,6 +816,7 @@
         outside(5, 1, "both")
         crossed(5, "own")
         guests(5, False)
+        chain(1, False)
         attention(1)
         crossed(6, "own")
         guests(6, False)
@@ -763,6 +828,7 @@
         relays(1)
         out_load.wait()
         settle(0)
+        worker_drain()
         relays(2)
 
     settle(1)
@@ -773,74 +839,15 @@
             for k in range(tp - 1):
                 normed_copy(u, i, col, k, pair_col).wait_send()
 
-    @pl.when(is_end)
-    def _():
-        for pieces in PHASES:
-            for piece in pieces:
-                copy(piece, me, send_own.at[piece, 1], peer).wait_send()
-                if piece in EARLY:
-                    copy(piece, me, send_own.at[piece, 0], peer).wait_send()
-                    copy(piece, peer, send_line.at[piece, peer], peer).wait_send()
-        for j in range(PARTS):
-            tok_copy(col * PARTS + j, j, 0, {"seq": partner}, True).wait_send()
-
     @pl.when(is_worker)
     def _():
-        def host_drain():
-            for j in range(PARTS):
-                for k in range(tp - 1):
-                    tok_copy(col * PARTS + j, j, k, {"tp": pair_col}).wait_send()
-
+        def run():
             @pl.loop(0, blocks)
             def _(i):
                 for u in range(len(units)):
                     guest_copy(u, i).wait_send()
 
-        hosts(host_drain)
-        for h in range(HALVES):
-
-            local_copy(h, 0, first_group).wait_send()
-            hosts(lambda: local_copy(h, 1, second_group).wait_send())
-
-            @pl.when(up_works)
-            def _():
-                line_state(h).wait_send()
-
-        for pieces in PHASES:
-            for piece in pieces:
-                copy(piece, me, send_own.at[piece, 0], peer).wait_send()
-
-                @pl.when(up_works)
-                def _():
-                    copy(piece, me, send_own.at[piece, 1], peer).wait_send()
-
-                @pl.when(down_works)
-                def _():
-                    copy(piece, me, send_own.at[piece, 2], peer).wait_send()
-
-                for origin, onward, _ in ends():
-                    source, other = origin * CROSS + b, origin * CROSS + (1 - b)
-
-                    @pl.when(onward)
-                    def _():
-                        copy(piece, source, send_line.at[piece, source], peer).wait_send()
-                        if piece in EARLY:
-                            copy(piece, other, send_line.at[piece, other], peer).wait_send()
-
-                    if piece not in EARLY:
-                        copy(piece, source, send_peer.at[piece, source], peer).wait_send()
-
-        def run(origin, onward, target):
-            source = origin * CROSS + b
-            for pieces in PHASES:
-                for piece in pieces:
-                    copy(piece, source, send_peer.at[piece, source], peer).wait_send()
-
-                    @pl.when(onward)
-                    def _():
-                        copy(piece, source, send_line.at[piece, source], peer).wait_send()
-
-        each_middle(run)
+        hosts(run)
 
 
 def on_device(

time: 135 us -> 134 us (level)
  no operation moved by 1% of the time
where the time goes in v1:
time: 134 us; the launch traced here: 133 us
  Pallas kernels  129 us (96%)
  local copies, waits for them, and re-layouts  4.17 us (3%)
    pallas_call x1, Pallas kernels, on_device(): pl.pallas_call(functools.partial(layer_kernel, seq, tp, heads, wide), out...  129 us
    unnamed x2, local copies, waits for them, and re-layouts  4.17 us

profile of v1, /device:TPU:0, one launch (start us, length us, event | category | flops | bytes accessed | tf_op | source)
XLA Modules:
  0.0 133.3 jit_solution(1790625429180786061)
XLA Ops:
  0.0 1.5 %copy.9.refs_3_ = bf16[512,4]{1,0:T(8,128)(2,1)} copy(bf16[512,4]{0,1:T(4,128)(2,1)} %param.12) | data formatting | bytes 8192 | tf_op args[4]
  1.5 129.1 %shard_map.82 = bf16[768,1024]{1,0:T(8,128)(2,1)} custom-call(bf16[768,4096]{1,0:T(8,128)(2,1)} %refs_0_.1, f32[4]{0:T(128)} %refs_1_.1, f32[1,512]{1,0:T(1,128)} %bitcast.1, bf16[512,4]{1,0:T(8,128)(2,1)} %copy.9.refs_3_, bf16[512,512]{1,0:T(8,128)(2,1)} %refs_4_.1, bf16[512,512]{1,0:T(8,128)(2,1)} %refs_5_.1, bf16[512,512]{1,0:T(8,128)(2,1)} %refs_6_.1, ...), custom_call_target="tpu_custom_call" | custom-call | tf_op jit(solution)/shard_map/pallas_call | solution.py:881
  130.6 2.7 %copy.11 = bf16[768,1024]{1,0:T(8,128)(2,1)} copy(bf16[768,1024]{1,0:T(8,128)(2,1)} %shard_map.82) | data formatting | bytes 3145728
